TPU v7x, 32 devices: a whole 2x2x4 slice. The times are simulated.
32 devices in a mesh: dp: 2 (over x), c: 4 (over z), r: 4 (over y, core).
Axes of the slice: x: 2, y: 2, z: 4, core: 2. Of those that a mesh axis runs over, the one named last changes fastest.
Arguments:
- x: bfloat16 [6144, 3584], P(('dp', 'r'), 'c'), parts along dimension 0
- w: bfloat16 [3584, 28672], P('r', 'c')
- dy: bfloat16 [6144, 28672], P(('dp', 'r'), 'c'), parts along dimension 0
Outputs:
- output 1: bfloat16 [6144, 3584], P(('dp', 'r'), 'c'), parts along dimension 0
- output 2: float32 [7168, 28672], P(('dp', 'r'), 'c'), parts along dimension 0
There are 2 independent parts. A program takes and returns all parts, laid end to end along the dimension named above; an argument that names none is the same for every part.
All inputs are finite; a program needn't handle non-finite values.
Results may differ from a plain program's by a relative error of at most 0.001.
Values are sent between devices in bfloat16 or wider.
A program may use at most 1 GiB of HBM per device.

v0:
```python
import jax
import jax.numpy as jnp
from jax import lax
from jax.sharding import PartitionSpec as P


def solution(mesh):
    def local(x, w, dy):
        w_col = lax.all_gather(w, "r", axis=0, tiled=True)
        dx_part = lax.dot_general(dy, w_col, (((1,), (1,)), ((), ())),
                                  preferred_element_type=jnp.float32)
        dx = lax.psum_scatter(dx_part, "c", scatter_dimension=1, tiled=True).astype(jnp.bfloat16)
        x_row = lax.all_gather(x, "c", axis=1, tiled=True)
        dw_part = lax.dot_general(x_row, dy, (((0,), (0,)), ((), ())),
                                  preferred_element_type=jnp.float32)
        dw = lax.psum_scatter(dw_part, "r", scatter_dimension=0, tiled=True)
        return dx, dw

    act = P(("dp", "r"), "c")
    return jax.shard_map(local, mesh=mesh, in_specs=(act, P("r", "c"), act),
                         out_specs=(act, act), check_vma=False)
```

profile of v0, /device:TPU:0, one launch (start us, length us, event | category | flops | bytes accessed | tf_op | source)
XLA Modules:
  0.0 1276.7 jit_solution(16083791797588532987)
XLA Ops:
  7.2 0.0 all-gather.3.cloned.1.call-start
  7.2 0.7 all-gather.3.cloned.1.call-update
  7.9 0.0 all-gather.5.cloned.1.call-start
  7.9 0.7 all-gather.5.cloned.1.call-update
  8.6 0.0 reduce-scatter.3.cloned.1.call-start
  8.7 309.0 %all-gather.3.cloned.1.call-done = bf16[3584,7168]{1,0:T(8,128)(2,1)} async-done(((bf16[896,7168]{1,0:T(8,128)(2,1)}), bf16[3584,7168]{1,0:T(8,128)(2,1)}) %all-gather.3.cloned.1.call-update) | async-done | bytes 51380240 | tf_op jit(solution)/shard_map/all_gather | solution.py:9
  317.7 48.5 %fusion = f32[768,3584]{1,0:T(8,128)} fusion(bf16[768,7168]{1,0:T(8,128)(2,1)} %param.5, bf16[3584,7168]{1,0:T(8,128)(2,1)} %all-gather.3.cloned.1.call-done), kind=kOutput, calls=%fused_computation | convolution fusion | flops 39460012032 | bytes 73400320 | tf_op jit(solution)/shard_map/dot_general | solution.py:10
  366.3 0.0 reduce-scatter.3.cloned.1.call-update
  366.3 0.0 reduce-scatter.5.cloned.1.call-start
  366.3 54.9 %all-gather.5.cloned.1.call-done = bf16[768,3584]{1,0:T(8,128)(2,1)} async-done(((bf16[768,896]{1,0:T(8,128)(2,1)}), bf16[768,3584]{1,0:T(8,128)(2,1)}) %all-gather.5.cloned.1.call-update) | async-done | bytes 5505040 | tf_op jit(solution)/shard_map/all_gather | solution.py:13
  421.2 49.9 %fusion.1 = f32[3584,7168]{1,0:T(8,128)} fusion(bf16[768,3584]{1,0:T(8,128)(2,1)} %all-gather.5.cloned.1.call-done, bf16[768,7168]{1,0:T(8,128)(2,1)} %param.5), kind=kOutput, calls=%fused_computation.1 | convolution fusion | flops 39460012032 | bytes 119275520 | tf_op jit(solution)/shard_map/dot_general | solution.py:14
  471.1 0.0 reduce-scatter.5.cloned.1.call-update
  471.2 137.3 %reduce-scatter.3.cloned.1.call-done = f32[768,896]{1,0:T(8,128)} async-done(((f32[768,3584]{1,0:T(8,128)}), f32[768,896]{1,0:T(8,128)}) %reduce-scatter.3.cloned.1.call-update) | async-done | bytes 2752528 | tf_op jit(solution)/shard_map/reduce_scatter | solution.py:12
  608.5 3.0 convert_element_type.3
  611.4 658.7 %reduce-scatter.5.cloned.1.call-done = f32[896,7168]{1,0:T(8,128)} async-done(((f32[3584,7168]{1,0:T(8,128)}), f32[896,7168]{1,0:T(8,128)}) %reduce-scatter.5.cloned.1.call-update) | async-done | bytes 25690128 | tf_op jit(solution)/shard_map/reduce_scatter | solution.py:16
Async XLA Ops:
  7.2 310.5 %all-gather.3.cloned.1.call-start = ((), (), s32[]{:S(2)}) async-start(), calls=%async_computation.2 | async-start | bytes 64225280 | tf_op jit(solution)/shard_map/all_gather | solution.py:9
  7.9 413.3 %all-gather.5.cloned.1.call-start = ((), (), s32[]{:S(2)}) async-start(), calls=%async_computation.4 | async-start | bytes 6881280 | tf_op jit(solution)/shard_map/all_gather | solution.py:13
  8.6 599.8 %reduce-scatter.3.cloned.1.call-start = ((), (), s32[]{:S(2)}) async-start(), calls=%async_computation.3 | async-start | bytes 13762560 | tf_op jit(solution)/shard_map/reduce_scatter | solution.py:12
  366.3 903.9 %reduce-scatter.5.cloned.1.call-start = ((), (), s32[]{:S(2)}) async-start(), calls=%async_computation.5 | async-start | bytes 128450560 | tf_op jit(solution)/shard_map/reduce_scatter | solution.py:16
Sparse Core Ops, SparseCore 0:
  9.5 308.1 all-gather.2
  319.3 101.8 all-gather.4
  423.6 184.8 reduce-scatter.2
  611.5 658.6 reduce-scatter.4
where the time goes:
time: 1280 us
  waiting for transfers between devices  1160 us (91%)
  matrix products  98.5 us (8%)
  between operations  13.8 us (1%)
    reduce_scatter x1, waiting for transfers between devices, local(): dw = lax.psum_scatter(dw_part, 'r', scatter_dimension=0, tiled=True)  659 us
    all_gather x1, waiting for transfers between devices, local(): w_col = lax.all_gather(w, 'r', axis=0, tiled=True)  309 us
    reduce_scatter x1, waiting for transfers between devices, local(): lax.psum_scatter(dx_part, 'c', scatter_dimension=1, tiled=True)  137 us
    all_gather x1, waiting for transfers between devices, local(): x_row = lax.all_gather(x, 'c', axis=1, tiled=True)  54.9 us
    dot_general x1, matrix products, local(): lax.dot_general(x_row, dy, (((0,), (0,)), ((), ())), preferred_element_ty...  49.9 us
    dot_general x1, matrix products, local(): lax.dot_general(dy, w_col, (((1,), (1,)), ((), ())), preferred_element_ty...  48.5 us
  transfers between devices with their start and end apart: 4, of which 4 were waited for; matrix products, arithmetic and copies ran while one was open for 8% of the time, Pallas kernels for 0%

commit v1 on v0

v1 whole, which is shorter than its diff:
```python
import jax
import jax.numpy as jnp
from jax import lax
from jax.experimental import pallas as pl
from jax.experimental.pallas import tpu as pltpu
from jax.sharding import PartitionSpec as P

N = 4
ANY = pl.BlockSpec(memory_space=pl.ANY)
PIECES = 12
CHUNKS = 2 * PIECES
THIRD = PIECES // 2


def exchange(xt_ref, w_ref, dy_ref, dx_ref, dyg_ref, xg_ref,
             wv, dyv, pv, upv, dnv, ov, xv,
             x_s, xu_s, xd_s, x_r, y_s, y_r, o_s, o_r, f_s, f_r, c_s, cu_r, cd_r, b_s, b_r, ld, aux):
    r = lax.axis_index("r")
    z = lax.axis_index("c")
    r1 = r + 1 - 2 * (r % 2)
    r2 = (r + 2) % N
    r3 = N - 1 - r
    mx = ((r // 2 + z // 2) % 2) * 2 + (r % 2 + z % 2) % 2
    diag = r == z
    has_up = jnp.logical_and(z >= r, z < N - 1)
    has_dn = jnp.logical_and(z <= r, z > 0)
    rows = dy_ref.shape[0]
    p = rows // PIECES
    n = w_ref.shape[1]
    kb = n // 7

    def far(src, dst, s, d, **where):
        return pltpu.make_async_remote_copy(src_ref=src, dst_ref=dst, send_sem=s, recv_sem=d, device_id=where,
                                            device_id_type=pl.DeviceIdType.MESH)

    def piece(q, cnt=1):
        return pl.ds(pl.multiple_of(q * p, p), cnt * p)

    barrier = pltpu.get_barrier_semaphore()
    for peer in (r1, r2, r3):
        pl.semaphore_signal(barrier, inc=1, device_id={"r": peer}, device_id_type=pl.DeviceIdType.MESH)

    @pl.when(z > 0)
    def _():
        pl.semaphore_signal(barrier, inc=1, device_id={"c": z - 1}, device_id_type=pl.DeviceIdType.MESH)

    @pl.when(z < N - 1)
    def _():
        pl.semaphore_signal(barrier, inc=1, device_id={"c": z + 1}, device_id_type=pl.DeviceIdType.MESH)

    pl.semaphore_wait(barrier, jnp.where(jnp.logical_or(z == 0, z == N - 1), 4, 5))

    def x_send():
        return far(xt_ref, xg_ref.at[mx], x_s.at[0], x_r.at[mx], r=z)

    def x_up(src, m):
        return far(src, xg_ref.at[m], xu_s.at[m], x_r.at[m], c=z + 1)

    def x_dn(src, m):
        return far(src, xg_ref.at[m], xd_s.at[m], x_r.at[m], c=z - 1)

    @pl.when(jnp.logical_not(diag))
    def _():
        x_send().start()

    def y_send(q):
        return far(dy_ref.at[piece(q)], dyg_ref.at[1, piece(q)], y_s.at[q], y_r.at[q], r=r2)

    def o_send(q):
        return far(dy_ref.at[piece(2 * q, 2)], dyg_ref.at[0, piece(2 * q, 2)], o_s.at[q], o_r.at[q], r=r1)

    def f_send(q):
        return far(dyg_ref.at[1, piece(q)], dyg_ref.at[2, piece(q)], f_s.at[q], f_r.at[q], r=r1)

    @pl.loop(0, PIECES)
    def _(q):
        y_send(q).start()

    w_load = pltpu.make_async_copy(w_ref, wv, aux.at[0])
    w_load.start()

    @pl.loop(0, THIRD)
    def _(q):
        o_send(q).start()

    @pl.when(diag)
    def _():
        cp = pltpu.make_async_copy(xt_ref, xv, aux.at[1])
        cp.start()

        @pl.when(z < N - 1)
        def _():
            x_up(xt_ref, 0).start()

        @pl.when(z > 0)
        def _():
            x_dn(xt_ref, 0).start()

        cp.wait()
        pltpu.make_async_copy(xv, xg_ref.at[0], aux.at[1]).start()

    w_load.wait()

    dist = jnp.abs(z - r)
    lag = jnp.where(z > r, N - 1 - z, jnp.where(z < r, z, jnp.maximum(z, N - 1 - z)))

    def x_step(c):
        for m in range(N):
            pos = jnp.where(dist == 0, 2 + m if m else -1, 3 * (m + dist))

            @pl.when(c == pos)
            def _():
                x_send_like = far(xt_ref, xg_ref.at[m], x_s.at[0], x_r.at[m], r=z)
                x_send_like.wait_recv()

                @pl.when(has_up)
                def _():
                    x_up(xg_ref.at[m], m).start()

                @pl.when(has_dn)
                def _():
                    x_dn(xg_ref.at[m], m).start()

    def f_step(q):
        y_send(q).wait_recv()
        f_send(q).start()

    def multiply(c, src0, src1):
        c0 = pltpu.make_async_copy(src0, dyv.at[pl.ds(0, p)], ld.at[0])
        c1 = pltpu.make_async_copy(src1, dyv.at[pl.ds(p, p)], ld.at[1])
        c0.start()
        c1.start()
        c0.wait()
        c1.wait()

        def part(i):
            s = pl.ds(pl.multiple_of(i * kb, kb), kb)
            return lax.dot_general(dyv[:, s], wv[:, s], (((1,), (1,)), ((), ())),
                                   preferred_element_type=jnp.float32)

        pv[c] = part(0)

        @pl.loop(1, 7)
        def _(i):
            pv[c] += part(i)

    def c_dn(c):
        return far(pv.at[c], upv.at[c], c_s.at[c], cu_r.at[c], c=z - 1)

    def c_up(c):
        return far(pv.at[c], dnv.at[c], c_s.at[c], cd_r.at[c], c=z + 1)

    def back(c, h, q, peer):
        return far(ov.at[c, pl.ds(h * p, p)], dx_ref.at[piece(q)], b_s.at[c, h], b_r.at[q], r=peer)

    def own_out(c):
        return pltpu.make_async_copy(ov.at[c], dx_ref.at[piece(2 * c, 2)], b_s.at[c, 0])

    def finish(c, start):
        def go(cp):
            if start:
                cp.start()
            else:
                cp.wait_send()

        @pl.when(c < THIRD)
        def _():
            if start:
                own_out(c).start()
            else:
                own_out(c).wait()

        @pl.when(jnp.logical_and(c >= THIRD, c < PIECES))
        def _():
            go(back(c, 0, 2 * (c - THIRD), r1))
            go(back(c, 1, 2 * (c - THIRD) + 1, r1))

        @pl.when(c >= PIECES)
        def _():
            go(back(c, 0, c - PIECES, r2))
            go(back(c, 1, c - PIECES, r3))

    def sum_step(c):
        @pl.when(has_up)
        def _():
            c_dn(c).wait_recv()
            pv[c] += upv[c]

        @pl.when(has_dn)
        def _():
            c_up(c).wait_recv()
            pv[c] += dnv[c]

        @pl.when(z > r)
        def _():
            c_dn(c).start()

        @pl.when(z < r)
        def _():
            c_up(c).start()

        @pl.when(diag)
        def _():
            ov[c] = pv[c].astype(jnp.bfloat16)
            finish(c, True)

    def after(c):
        x_step(c)

        @pl.when(c >= lag)
        def _():
            sum_step(c - lag)

    @pl.loop(0, PIECES)
    def _(c):
        @pl.when(jnp.logical_and(c >= 6, c % 2 == 0))
        def _():
            f_step((c - 6) // 2)

        @pl.when(c < THIRD)
        def _():
            multiply(c, dy_ref.at[piece(2 * c)], dy_ref.at[piece(2 * c + 1)])

        @pl.when(c >= THIRD)
        def _():
            i = c - THIRD
            o_send(i).wait_recv()
            multiply(c, dyg_ref.at[0, piece(2 * i)], dyg_ref.at[0, piece(2 * i + 1)])

        after(c)

    @pl.loop(PIECES, CHUNKS)
    def _(c):
        q = c - PIECES

        @pl.when(jnp.logical_and(c < 18, c % 2 == 0))
        def _():
            f_step((c - 6) // 2)

        @pl.when(c >= 18)
        def _():
            f_step(q)

        f_send(q).wait_recv()
        multiply(c, dyg_ref.at[1, piece(q)], dyg_ref.at[2, piece(q)])
        after(c)

    @pl.loop(0, N - 1)
    def _(i):
        @pl.when(i < lag)
        def _():
            sum_step(CHUNKS - lag + i)

    @pl.when(jnp.logical_not(diag))
    def _():
        x_send().wait_send()

        @pl.loop(0, CHUNKS)
        def _(c):
            c_dn(c).wait_send()

        @pl.loop(0, PIECES)
        def _(q):
            back(0, 0, q, r1).wait_recv()

    @pl.when(diag)
    def _():
        pltpu.make_async_copy(xv, xg_ref.at[0], aux.at[1]).wait()

        @pl.loop(0, CHUNKS)
        def _(c):
            finish(c, False)

    for m in range(N):
        @pl.when(has_up)
        def _():
            x_up(xg_ref.at[m], m).wait_send()

        @pl.when(has_dn)
        def _():
            x_dn(xg_ref.at[m], m).wait_send()

    @pl.loop(0, PIECES)
    def _(q):
        y_send(q).wait_send()
        f_send(q).wait_send()

    @pl.loop(0, THIRD)
    def _(q):
        o_send(q).wait_send()


def weight_grad(xg, dy, dyg):
    rows, n = dy.shape
    k = xg.shape[1]
    bn = n // 14

    def body(x_ref, d_ref, g_ref, o_ref):
        tot = jnp.dot(x_ref[0], d_ref[...], preferred_element_type=jnp.float32)
        for m in range(1, N):
            tot += jnp.dot(x_ref[m], g_ref[m - 1], preferred_element_type=jnp.float32)
        o_ref[...] = tot

    return pl.pallas_call(
        body,
        grid=(n // bn,),
        in_specs=[pl.BlockSpec(xg.shape, lambda i: (0, 0, 0)),
                  pl.BlockSpec((rows, bn), lambda i: (0, i)),
                  pl.BlockSpec((N - 1, rows, bn), lambda i: (0, 0, i))],
        out_specs=pl.BlockSpec((k, bn), lambda i: (0, i)),
        out_shape=jax.ShapeDtypeStruct((k, n), jnp.float32),
        compiler_params=pltpu.CompilerParams(vmem_limit_bytes=48 << 20),
        cost_estimate=pl.CostEstimate(flops=2 * N * rows * k * n, bytes_accessed=8 * rows * n + 4 * k * n,
                                      transcendentals=0),
        name="weight_grad",
    )(xg, dy, dyg)


def solution(mesh):
    def local(x, w, dy):
        xt = x.T
        rows, n = dy.shape
        k = w.shape[0]
        p = rows // PIECES
        dma = pltpu.SemaphoreType.DMA
        bf, f32 = jnp.bfloat16, jnp.float32
        dx, dyg, xg = pl.pallas_call(
            exchange,
            in_specs=[ANY] * 3,
            out_specs=[ANY] * 3,
            out_shape=[jax.ShapeDtypeStruct((rows, k), bf),
                       jax.ShapeDtypeStruct((N - 1, rows, n), bf),
                       jax.ShapeDtypeStruct((N, k, rows), bf)],
            scratch_shapes=[
                pltpu.VMEM((k, n), bf), pltpu.VMEM((2 * p, n), bf),
                pltpu.VMEM((CHUNKS, 2 * p, k), f32), pltpu.VMEM((CHUNKS, 2 * p, k), f32),
                pltpu.VMEM((CHUNKS, 2 * p, k), f32), pltpu.VMEM((CHUNKS, 2 * p, k), bf), pltpu.VMEM((k, rows), bf),
                dma((1,)), dma((N,)), dma((N,)), dma((N,)),
                dma((PIECES,)), dma((PIECES,)), dma((THIRD,)), dma((THIRD,)), dma((PIECES,)), dma((PIECES,)),
                dma((CHUNKS,)), dma((CHUNKS,)), dma((CHUNKS,)), dma((CHUNKS, 2)), dma((PIECES,)), dma((2,)), dma((2,)),
            ],
            compiler_params=pltpu.CompilerParams(collective_id=0, has_side_effects=True, vmem_limit_bytes=67043328),
            cost_estimate=pl.CostEstimate(flops=8 * rows * k * n, bytes_accessed=16 * rows * n, transcendentals=0),
            name="exchange",
        )(xt, w, dy)
        return dx, weight_grad(xg, dy, dyg)

    act = P(("dp", "r"), "c")
    return jax.shard_map(local, mesh=mesh, in_specs=(act, P("r", "c"), act),
                         out_specs=(act, act), check_vma=False)
```

time: 1280 us -> 355 us (0.28)
  waiting for transfers between devices: 1160 us -> 0 us
  Pallas kernels: 0 us -> 347 us
  matrix products: 98.5 us -> 0 us
  between operations: 13.8 us -> 0.65 us
    reduce_scatter x2 -> x0, waiting for transfers between devices: 796 us -> none  [the longest x1 659 us: local(): dw = lax.psum_scatter(dw_part, 'r', scatter_dimension=0, tiled=True)]
    all_gather x2 -> x0, waiting for transfers between devices: 364 us -> none  [the longest x1 309 us: local(): w_col = lax.all_gather(w, 'r', axis=0, tiled=True)]
    pallas_call x0 -> x2, Pallas kernels: none -> 347 us  [the longest x1 301 us: local(): pl.pallas_call(exchange, in_specs=[ANY] * 3, out_specs=[ANY] * 3, out_sha...]
    dot_general x2 -> x0, matrix products: 98.5 us -> none  [the longest x1 49.9 us: local(): lax.dot_general(x_row, dy, (((0,), (0,)), ((), ())), preferred_element_ty...]
  transfers between devices with their start and end apart: 4 -> 0, of which waited for: 4 -> 0; matrix products, arithmetic and copies ran while one was open for 8% -> 0% of each run, Pallas kernels for 0% -> 0%
where the time goes in v1:
time: 355 us; the launch traced here: 354 us
  Pallas kernels  347 us (98%)
  local copies, waits for them, and re-layouts  6.14 us (2%)
    pallas_call x1, Pallas kernels, local(): pl.pallas_call(exchange, in_specs=[ANY] * 3, out_specs=[ANY] * 3, out_sha...  301 us
    pallas_call x1, Pallas kernels, weight_grad(): pl.pallas_call(body, grid=(n // bn,), in_specs=[pl.BlockSpec(xg.shape, la...  45.4 us

profile of v1, /device:TPU:0, one launch (start us, length us, event | category | flops | bytes accessed | tf_op | source)
XLA Modules:
  0.0 353.6 jit_solution(14502389253246359264)
XLA Ops:
  0.6 2.5 copy.5
  3.1 301.4 %exchange.1 = (bf16[768,896]{1,0:T(8,128)(2,1)}, bf16[3,768,7168]{2,1,0:T(8,128)(2,1)}, bf16[4,896,768]{2,1,0:T(8,128)(2,1)}) custom-call(bf16[896,768]{1,0:T(8,128)(2,1)} %bitcast.1, bf16[896,7168]{1,0:T(8,128)(2,1)} %w_ref.1, bf16[768,7168]{1,0:T(8,128)(2,1)} %d_ref.1), custom_call_target="tpu_custom_call" | custom-call | flops 39460012032 | bytes 88080384 | tf_op jit(solution)/shard_map/exchange/pallas_call | solution.py:327
  304.6 0.0 copy-start
  304.6 2.6 copy-done
  307.1 0.0 copy-start.1
  307.1 45.4 %weight_grad.1 = f32[896,7168]{1,0:T(8,128)} custom-call(bf16[4,896,768]{2,1,0:T(8,128)(2,1)S(1)} %copy-done, bf16[768,7168]{1,0:T(8,128)(2,1)} %d_ref.1, bf16[3,768,7168]{2,1,0:T(8,128)(2,1)} %get-tuple-element.7.g_ref), custom_call_target="tpu_custom_call" | custom-call | flops 39460012032 | bytes 69730304 | tf_op jit(solution)/shard_map/weight_grad/pallas_call | solution.py:304
  352.6 0.0 copy-done.1
  352.6 1.1 copy.7
Async XLA Ops:
  304.6 2.6 copy-start
  307.1 45.4 %copy-start.1 = (bf16[768,896]{1,0:T(8,128)(2,1)S(1)}, bf16[768,896]{1,0:T(8,128)(2,1)}, u32[]{:S(2)}) copy-start(bf16[768,896]{1,0:T(8,128)(2,1)} %get-tuple-element.10) | copy-start | bytes 4128772

commit v2 on v1

v2 whole, which is shorter than its diff:
```python
import jax
import jax.numpy as jnp
from jax import lax
from jax.experimental import pallas as pl
from jax.experimental.pallas import tpu as pltpu
from jax.sharding import PartitionSpec as P

N = 4
ANY = pl.BlockSpec(memory_space=pl.ANY)
PIECES = 12
PARTS = PIECES + 1
CHUNKS = 2 * PIECES
LAST = CHUNKS - 1
THIRD = PIECES // 2
UNITS = 28
PER = 3


def exchange(xt_ref, w_ref, dy_ref, dx_ref, dyg_ref, xg_ref, dwp_ref,
             wv, dyv, pv, upv, dnv, ov, xr, db, ob,
             x_s, xu_s, xd_s, x_r, y_s, y_r, o_s, o_r, f_s, f_r, c_s, cu_r, cd_r, b_s, b_r, ld, u_s, v_s, aux):
    r = lax.axis_index("r")
    z = lax.axis_index("c")
    r1 = r + 1 - 2 * (r % 2)
    r2 = (r + 2) % N
    r3 = N - 1 - r
    mx = ((r // 2 + z // 2) % 2) * 2 + (r % 2 + z % 2) % 2
    diag = r == z
    has_up = jnp.logical_and(z >= r, z < N - 1)
    has_dn = jnp.logical_and(z <= r, z > 0)
    rows = dy_ref.shape[0]
    p = rows // PIECES
    n = w_ref.shape[1]
    kb = n // 7

    def far(src, dst, s, d, **where):
        return pltpu.make_async_remote_copy(src_ref=src, dst_ref=dst, send_sem=s, recv_sem=d, device_id=where,
                                            device_id_type=pl.DeviceIdType.MESH)

    def piece(q, cnt=1):
        return pl.ds(pl.multiple_of(q * p, p), cnt * p)

    def half(j):
        return pl.ds((PIECES - 1) * p + j * (p // 2), p // 2)

    def where_rows(q):
        return half(q - PIECES + 1) if isinstance(q, int) and q >= PIECES - 1 else piece(q)

    barrier = pltpu.get_barrier_semaphore()
    for peer in (r1, r2, r3):
        pl.semaphore_signal(barrier, inc=1, device_id={"r": peer}, device_id_type=pl.DeviceIdType.MESH)

    @pl.when(z > 0)
    def _():
        pl.semaphore_signal(barrier, inc=1, device_id={"c": z - 1}, device_id_type=pl.DeviceIdType.MESH)

    @pl.when(z < N - 1)
    def _():
        pl.semaphore_signal(barrier, inc=1, device_id={"c": z + 1}, device_id_type=pl.DeviceIdType.MESH)

    pl.semaphore_wait(barrier, jnp.where(jnp.logical_or(z == 0, z == N - 1), 4, 5))

    def x_send():
        return far(xt_ref, xg_ref.at[mx], x_s.at[0], x_r.at[mx], r=z)

    def x_up(src, m):
        return far(src, xg_ref.at[m], xu_s.at[m], x_r.at[m], c=z + 1)

    def x_dn(src, m):
        return far(src, xg_ref.at[m], xd_s.at[m], x_r.at[m], c=z - 1)

    @pl.when(jnp.logical_not(diag))
    def _():
        x_send().start()

    def y_send(q):
        return far(dy_ref.at[where_rows(q)], dyg_ref.at[1, where_rows(q)], y_s.at[q], y_r.at[q], r=r2)

    def o_send(q):
        return far(dy_ref.at[piece(2 * q, 2)], dyg_ref.at[0, piece(2 * q, 2)], o_s.at[q], o_r.at[q], r=r1)

    def f_send(q):
        return far(dyg_ref.at[1, where_rows(q)], dyg_ref.at[2, where_rows(q)], f_s.at[q], f_r.at[q], r=r1)

    @pl.loop(0, PIECES - 1)
    def _(q):
        y_send(q).start()

    for q in (PIECES - 1, PIECES):
        y_send(q).start()

    w_load = pltpu.make_async_copy(w_ref, wv, aux.at[0])
    w_load.start()

    @pl.loop(0, THIRD)
    def _(q):
        o_send(q).start()

    @pl.when(diag)
    def _():
        cp = pltpu.make_async_copy(xt_ref, xr.at[:, pl.ds(0, rows)], aux.at[1])
        cp.start()

        @pl.when(z < N - 1)
        def _():
            x_up(xt_ref, 0).start()

        @pl.when(z > 0)
        def _():
            x_dn(xt_ref, 0).start()

        cp.wait()
        cp = pltpu.make_async_copy(xr.at[:, pl.ds(0, rows)], xg_ref.at[0], aux.at[1])
        cp.start()
        cp.wait()

    w_load.wait()

    dist = jnp.abs(z - r)
    lag = jnp.where(z > r, N - 1 - z, jnp.where(z < r, z, jnp.maximum(z, N - 1 - z)))

    def x_step(c):
        for m in range(N):
            pos = jnp.where(dist == 0, (-1, 3, 6, 7)[m], 3 * (m + dist) + (2 if m > 1 else -1))

            @pl.when(c == pos)
            def _():
                x_send_like = far(xt_ref, xg_ref.at[m], x_s.at[0], x_r.at[m], r=z)
                x_send_like.wait_recv()

                @pl.when(has_up)
                def _():
                    x_up(xg_ref.at[m], m).start()

                @pl.when(has_dn)
                def _():
                    x_dn(xg_ref.at[m], m).start()

    def f_step(q):
        y_send(q).wait_recv()
        f_send(q).start()

    def load_pair(i):
        return pltpu.make_async_copy(dy_ref.at[piece(4 * i, 4)], dyv, ld.at[0])

    def load_other(i):
        return pltpu.make_async_copy(dyg_ref.at[0, piece(4 * i, 4)], dyv, ld.at[0])

    def load_far(q, size):
        return [pltpu.make_async_copy(dyg_ref.at[1 + h, where_rows(q)], dyv.at[pl.ds(h * size, size)], ld.at[h])
                for h in (0, 1)]

    def product(dsts, size):
        def part(i):
            s = pl.ds(pl.multiple_of(i * kb, kb), kb)
            return lax.dot_general(dyv[:len(dsts) * size, s], wv[:, s], (((1,), (1,)), ((), ())),
                                   preferred_element_type=jnp.float32)

        first = part(0)
        for j, d in enumerate(dsts):
            d[...] = first[j * size:(j + 1) * size]

        @pl.loop(1, 7)
        def _(i):
            t = part(i)
            for j, d in enumerate(dsts):
                d[...] += t[j * size:(j + 1) * size]

    def rows_of(ref, c):
        if isinstance(c, int) and c >= LAST:
            return ref.at[LAST, pl.ds((c - LAST) * p, p)]
        return ref.at[c]

    def by_size(c, fn):
        @pl.when(c < LAST)
        def _():
            fn(c)

        for j in (LAST, LAST + 1):
            @pl.when(c == j)
            def _():
                fn(j)

    def c_dn(c):
        return far(rows_of(pv, c), rows_of(upv, c), c_s.at[c], cu_r.at[c], c=z - 1)

    def c_up(c):
        return far(rows_of(pv, c), rows_of(dnv, c), c_s.at[c], cd_r.at[c], c=z + 1)

    def back(c, h, q, peer, off, size):
        return far(ov.at[min(c, LAST) if isinstance(c, int) else c, pl.ds(off, size)], dx_ref.at[where_rows(q)],
                   b_s.at[c, h], b_r.at[q], r=peer)

    def own_out(c):
        return pltpu.make_async_copy(ov.at[c], dx_ref.at[piece(2 * c, 2)], b_s.at[c, 0])

    def finish(c, start):
        def go(cp):
            if start:
                cp.start()
            else:
                cp.wait_send()

        if isinstance(c, int):
            q, off, h = c - PIECES, (c - LAST) * p, p // 2
            go(back(c, 0, q, r2, off, h))
            go(back(c, 1, q, r3, off + h, h))
            return

        @pl.when(c < THIRD)
        def _():
            if start:
                own_out(c).start()
            else:
                own_out(c).wait()

        @pl.when(jnp.logical_and(c >= THIRD, c < PIECES - 1))
        def _():
            go(back(c, 0, 2 * (c - THIRD), r1, 0, p))
            go(back(c, 1, 2 * (c - THIRD) + 1, r1, p, p))

        @pl.when(c == PIECES - 1)
        def _():
            go(back(PIECES - 1, 0, PIECES - 2, r1, 0, p))
            go(back(PIECES - 1, 1, PIECES - 1, r1, p, p // 2))
            go(back(PIECES - 1, 2, PIECES, r1, p + p // 2, p // 2))

        @pl.when(c >= PIECES)
        def _():
            go(back(c, 0, c - PIECES, r2, 0, p))
            go(back(c, 1, c - PIECES, r3, p, p))

    def sum_one(c):
        mine = rows_of(pv, c)

        @pl.when(has_up)
        def _():
            c_dn(c).wait_recv()
            mine[...] += rows_of(upv, c)[...]

        @pl.when(has_dn)
        def _():
            c_up(c).wait_recv()
            mine[...] += rows_of(dnv, c)[...]

        @pl.when(z > r)
        def _():
            c_dn(c).start()

        @pl.when(z < r)
        def _():
            c_up(c).start()

        @pl.when(diag)
        def _():
            rows_of(ov, c)[...] = mine[...].astype(jnp.bfloat16)
            finish(c, True)

    def sum_step(c):
        by_size(c, sum_one)

    ub = n // UNITS
    spans = ((0, rows), (rows, rows))

    def xr_load(m):
        o, cnt = spans[m]
        return pltpu.make_async_copy(xg_ref.at[m, :, pl.ds(0, cnt)], xr.at[:, pl.ds(o, cnt)], v_s.at[m])

    def unit_load(u, m):
        o, cnt = spans[m]
        cols = pl.ds(pl.multiple_of(u * ub, ub), ub)
        src = dy_ref.at[:, cols] if m == 0 else dyg_ref.at[m - 1, :, cols]
        return pltpu.make_async_copy(src, db.at[u % 2, pl.ds(o, cnt)], u_s.at[u % 2, m])

    def unit_out(u):
        cols = pl.ds(pl.multiple_of(u * ub, ub), ub)
        return pltpu.make_async_copy(ob.at[u % 2], dwp_ref.at[:, cols], u_s.at[u % 2, 2])

    def unit(u):
        @pl.when(u == 0)
        def _():
            for m in range(2):
                xr_load(m).start()
                unit_load(0, m).start()
            for m in range(2):
                xr_load(m).wait()

        @pl.when(u + 1 < UNITS)
        def _():
            for m in range(2):
                unit_load(u + 1, m).start()

        for m in range(2):
            unit_load(u, m).wait()

        @pl.when(u >= 2)
        def _():
            unit_out(u - 2).wait()

        ob[u % 2] = jnp.dot(xr[...], db[u % 2], preferred_element_type=jnp.float32)
        unit_out(u).start()

    def after(c):
        @pl.when(c >= lag)
        def _():
            sum_step(c - lag)

    base = jnp.where(r // 2 == z // 2, 6, 3)
    ahead = PIECES - base

    def f_early(c):
        @pl.when(jnp.logical_and(c >= base, (c - base) % 2 == 0))
        def _():
            q = (c - base) // 2

            @pl.when(q <= ahead)
            def _():
                f_step(q)

    u0 = jnp.where(dist == 0, 4, 3 * (1 + dist))

    def units(c):
        @pl.when(c >= u0)
        def _():
            @pl.loop(0, PER)
            def _(i):
                u = (c - u0) * PER + i

                @pl.when(u < UNITS)
                def _():
                    unit(u)

    load_pair(0).start()

    @pl.loop(0, THIRD)
    def _(i):
        c = 2 * i
        f_early(c)
        load_pair(0).wait()
        product([pv.at[c], pv.at[c + 1]], 2 * p)

        @pl.when(i + 1 < THIRD // 2)
        def _():
            load_pair(i + 1).start()

        @pl.when(jnp.logical_and(i + 1 >= THIRD // 2, i + 1 < THIRD))
        def _():
            k = i + 1 - THIRD // 2

            @pl.when(k == 0)
            def _():
                @pl.loop(0, THIRD)
                def _(q):
                    o_send(q).wait_recv()

            load_other(k).start()

        x_step(c)
        after(c)
        units(c)
        f_early(c + 1)
        x_step(c + 1)
        after(c + 1)
        units(c + 1)

    @pl.loop(PIECES, LAST)
    def _(c):
        q = c - PIECES
        f_early(c)

        @pl.when(q > ahead)
        def _():
            f_step(q)

        f_send(q).wait_recv()
        for cp in load_far(q, p):
            cp.start()
        for cp in load_far(q, p):
            cp.wait()
        product([pv.at[c]], 2 * p)
        x_step(c)
        after(c)
        units(c)

    for c in (LAST, LAST + 1):
        q = c - PIECES
        f_step(q)
        f_send(q).wait_recv()
        for cp in load_far(q, p // 2):
            cp.start()
        for cp in load_far(q, p // 2):
            cp.wait()
        product([rows_of(pv, c)], p)
        sum_step(c - lag)

    @pl.loop(0, N - 1)
    def _(i):
        @pl.when(i < lag)
        def _():
            sum_step(CHUNKS + 1 - lag + i)

    for u in (UNITS - 2, UNITS - 1):
        unit_out(u).wait()

    @pl.when(jnp.logical_not(diag))
    def _():
        x_send().wait_send()

        @pl.loop(0, LAST)
        def _(c):
            c_dn(c).wait_send()

        for c in (LAST, LAST + 1):
            c_dn(c).wait_send()

        @pl.loop(0, PIECES - 1)
        def _(q):
            back(0, 0, q, r1, 0, p).wait_recv()

        for q in (PIECES - 1, PIECES):
            back(0, 0, q, r1, 0, p // 2).wait_recv()

    @pl.when(diag)
    def _():
        @pl.loop(0, LAST)
        def _(c):
            finish(c, False)

        for c in (LAST, LAST + 1):
            finish(c, False)

    for m in range(N):
        @pl.when(has_up)
        def _():
            x_up(xg_ref.at[m], m).wait_send()

        @pl.when(has_dn)
        def _():
            x_dn(xg_ref.at[m], m).wait_send()

    @pl.loop(0, PIECES - 1)
    def _(q):
        y_send(q).wait_send()
        f_send(q).wait_send()

    for q in (PIECES - 1, PIECES):
        y_send(q).wait_send()
        f_send(q).wait_send()

    @pl.loop(0, THIRD)
    def _(q):
        o_send(q).wait_send()


BLOCKS = 14
SLOTS = 6


def finish_grads(xg_ref, dyg_ref, dwp_ref, dxp_ref, dw_ref, dx_ref, xr, db, ob, dv, x_s, l_s, o_s, d_s):
    rows = dyg_ref.shape[1]
    bn = dw_ref.shape[1] // BLOCKS
    ahead = SLOTS - 2

    def load(u, h):
        cols, s = pl.ds(pl.multiple_of(u * bn, bn), bn), lax.rem(u, SLOTS)
        if h == 2:
            return pltpu.make_async_copy(dwp_ref.at[:, cols], ob.at[s], l_s.at[s, 2])
        return pltpu.make_async_copy(dyg_ref.at[1 + h, :, cols], db.at[s, pl.ds(h * rows, rows)], l_s.at[s, h])

    def out(u):
        cols, s = pl.ds(pl.multiple_of(u * bn, bn), bn), lax.rem(u, SLOTS)
        return pltpu.make_async_copy(ob.at[s], dw_ref.at[:, cols], o_s.at[s])

    xs = [pltpu.make_async_copy(xg_ref.at[2 + h], xr.at[:, pl.ds(h * rows, rows)], x_s.at[h]) for h in (0, 1)]
    d_in = pltpu.make_async_copy(dxp_ref, dv, d_s.at[0])
    d_out = pltpu.make_async_copy(dv, dx_ref, d_s.at[1])
    for cp in xs:
        cp.start()

    @pl.loop(0, ahead)
    def _(u):
        for h in range(3):
            load(u, h).start()

    d_in.start()
    for cp in xs:
        cp.wait()

    @pl.loop(0, BLOCKS)
    def _(u):
        @pl.when(u >= 2)
        def _():
            out(u - 2).wait()

        @pl.when(u + ahead < BLOCKS)
        def _():
            for h in range(3):
                load(u + ahead, h).start()

        for h in range(3):
            load(u, h).wait()
        s = lax.rem(u, SLOTS)
        ob[s] += jnp.dot(xr[...], db[s], preferred_element_type=jnp.float32)
        out(u).start()

        @pl.when(u == 2)
        def _():
            d_in.wait()
            d_out.start()

    out(BLOCKS - 2).wait()
    out(BLOCKS - 1).wait()
    d_out.wait()


def solution(mesh):
    def local(x, w, dy):
        xt = x.T
        rows, n = dy.shape
        k = w.shape[0]
        p = rows // PIECES
        dma = pltpu.SemaphoreType.DMA
        bf, f32 = jnp.bfloat16, jnp.float32
        dx, dyg, xg, dwp = pl.pallas_call(
            exchange,
            in_specs=[ANY] * 3,
            out_specs=[ANY] * 4,
            out_shape=[jax.ShapeDtypeStruct((rows, k), bf),
                       jax.ShapeDtypeStruct((N - 1, rows, n), bf),
                       jax.ShapeDtypeStruct((N, k, rows), bf),
                       jax.ShapeDtypeStruct((k, n), f32)],
            scratch_shapes=[
                pltpu.VMEM((k, n), bf), pltpu.VMEM((4 * p, n), bf),
                pltpu.VMEM((CHUNKS, 2 * p, k), f32), pltpu.VMEM((CHUNKS, 2 * p, k), f32),
                pltpu.VMEM((CHUNKS, 2 * p, k), f32), pltpu.VMEM((CHUNKS, 2 * p, k), bf),
                pltpu.VMEM((k, 2 * rows), bf),
                pltpu.VMEM((2, 2 * rows, n // UNITS), bf), pltpu.VMEM((2, k, n // UNITS), f32),
                dma((1,)), dma((N,)), dma((N,)), dma((N,)),
                dma((PARTS,)), dma((PARTS,)), dma((THIRD,)), dma((THIRD,)), dma((PARTS,)), dma((PARTS,)),
                dma((CHUNKS + 1,)), dma((CHUNKS + 1,)), dma((CHUNKS + 1,)), dma((CHUNKS + 1, 3)), dma((PARTS,)),
                dma((2,)), dma((2, 3)), dma((2,)), dma((2,)),
            ],
            compiler_params=pltpu.CompilerParams(collective_id=0, has_side_effects=True, vmem_limit_bytes=67043328),
            cost_estimate=pl.CostEstimate(flops=8 * rows * k * n, bytes_accessed=16 * rows * n, transcendentals=0),
            name="exchange",
        )(xt, w, dy)
        dw, dx = pl.pallas_call(
            finish_grads,
            in_specs=[ANY] * 4,
            out_specs=[ANY] * 2,
            out_shape=[jax.ShapeDtypeStruct((k, n), f32), jax.ShapeDtypeStruct((rows, k), bf)],
            scratch_shapes=[pltpu.VMEM((k, 2 * rows), bf), pltpu.VMEM((SLOTS, 2 * rows, n // BLOCKS), bf),
                            pltpu.VMEM((SLOTS, k, n // BLOCKS), f32), pltpu.VMEM((rows, k), bf),
                            dma((2,)), dma((SLOTS, 3)), dma((SLOTS,)), dma((2,))],
            compiler_params=pltpu.CompilerParams(vmem_limit_bytes=67043328),
            cost_estimate=pl.CostEstimate(flops=4 * rows * k * n, bytes_accessed=4 * rows * n + 8 * k * n,
                                          transcendentals=0),
            name="finish_grads",
        )(xg, dyg, dwp, dx)
        return dx, dw

    act = P(("dp", "r"), "c")
    return jax.shard_map(local, mesh=mesh, in_specs=(act, P("r", "c"), act),
                         out_specs=(act, act), check_vma=False)
```

time: 355 us -> 326 us (0.918)
  Pallas kernels: 347 us -> 322 us
  local copies, waits for them, and re-layouts: 6.14 us -> 2.51 us
    pallas_call x2, Pallas kernels: 347 us -> 322 us  [the longest x1 295 us: local(): pl.pallas_call(exchange, in_specs=[ANY] * 3, out_specs=[ANY] * 4, out_sha...]
    unnamed x6 -> x1, local copies, waits for them, and re-layouts: 6.14 us -> 2.51 us
where the time goes in v2:
time: 326 us; the launch traced here: 325 us
  Pallas kernels  322 us (99%)
    pallas_call x1, Pallas kernels, local(): pl.pallas_call(exchange, in_specs=[ANY] * 3, out_specs=[ANY] * 4, out_sha...  295 us
    pallas_call x1, Pallas kernels, local(): pl.pallas_call(finish_grads, in_specs=[ANY] * 4, out_specs=[ANY] * 2, out...  27.5 us

profile of v2, /device:TPU:0, one launch (start us, length us, event | category | flops | bytes accessed | tf_op | source)
XLA Modules:
  0.0 325.2 jit_solution(5035301117172886413)
XLA Ops:
  0.6 2.5 copy.5
  3.1 294.5 %exchange.1 = (bf16[768,896]{1,0:T(8,128)(2,1)}, bf16[3,768,7168]{2,1,0:T(8,128)(2,1)}, bf16[4,896,768]{2,1,0:T(8,128)(2,1)}, f32[896,7168]{1,0:T(8,128)}) custom-call(bf16[896,768]{1,0:T(8,128)(2,1)} %bitcast.1, bf16[896,7168]{1,0:T(8,128)(2,1)} %w_ref.1, bf16[768,7168]{1,0:T(8,128)(2,1)} %dy_ref.1), custom_call_target="tpu_custom_call" | custom-call | flops 39460012032 | bytes 88080384 | tf_op jit(solution)/shard_map/exchange/pallas_call | solution.py:524
  297.7 27.5 %finish_grads.1 = (f32[896,7168]{1,0:T(8,128)}, bf16[768,896]{1,0:T(8,128)(2,1)}) custom-call(bf16[4,896,768]{2,1,0:T(8,128)(2,1)} %get-tuple-element.8.xg_ref, bf16[3,768,7168]{2,1,0:T(8,128)(2,1)} %get-tuple-element.9.dyg_ref, f32[896,7168]{1,0:T(8,128)} %get-tuple-element.10.dwp_ref, bf16[768,896]{1,0:T(8,128)(2,1)} %get-tuple-element.11.dxp_ref), custom_call_target="tpu_custom_call" | custom-call | flops 19730006016 | bytes 73400320 | tf_op jit(solution)/shard_map/finish_grads/pallas_call | solution.py:547

commit v3 on v2

--- a/solution.py
+++ b/solution.py
@@ -13,10 +13,10 @@
 LAST = CHUNKS - 1
 THIRD = PIECES // 2
 UNITS = 28
-PER = 3
-
-
-def exchange(xt_ref, w_ref, dy_ref, dx_ref, dyg_ref, xg_ref, dwp_ref,
+PER = 4
+
+
+def exchange(x_ref, w_ref, dy_ref, dx_ref, dyg_ref, xg_ref, dwp_ref, xt_ref,
              wv, dyv, pv, upv, dnv, ov, xr, db, ob,
              x_s, xu_s, xd_s, x_r, y_s, y_r, o_s, o_r, f_s, f_r, c_s, cu_r, cd_r, b_s, b_r, ld, u_s, v_s, aux):
     r = lax.axis_index("r")
@@ -31,7 +31,6 @@
     rows = dy_ref.shape[0]
     p = rows // PIECES
     n = w_ref.shape[1]
-    kb = n // 7
 
     def far(src, dst, s, d, **where):
         return pltpu.make_async_remote_copy(src_ref=src, dst_ref=dst, send_sem=s, recv_sem=d, device_id=where,
@@ -69,10 +68,6 @@
     def x_dn(src, m):
         return far(src, xg_ref.at[m], xd_s.at[m], x_r.at[m], c=z - 1)
 
-    @pl.when(jnp.logical_not(diag))
-    def _():
-        x_send().start()
-
     def y_send(q):
         return far(dy_ref.at[where_rows(q)], dyg_ref.at[1, where_rows(q)], y_s.at[q], y_r.at[q], r=r2)
 
@@ -82,15 +77,29 @@
     def f_send(q):
         return far(dyg_ref.at[1, where_rows(q)], dyg_ref.at[2, where_rows(q)], f_s.at[q], f_r.at[q], r=r1)
 
-    @pl.loop(0, PIECES - 1)
+    y_send(0).start()
+    x_rows = x_ref.shape[0]
+    x_load = pltpu.make_async_copy(x_ref, ov.at[pl.ds(0, x_rows)], aux.at[1])
+    x_load.start()
+    w_load = pltpu.make_async_copy(w_ref, wv, aux.at[0])
+    w_load.start()
+    x_load.wait()
+    for j in range(x_rows):
+        xr[:, pl.ds(j * 2 * p, 2 * p)] = ov[j].T
+    x_store = pltpu.make_async_copy(xr.at[:, pl.ds(0, rows)], xt_ref, aux.at[1])
+    x_store.start()
+    x_store.wait()
+
+    @pl.when(jnp.logical_not(diag))
+    def _():
+        x_send().start()
+
+    @pl.loop(1, PIECES - 1)
     def _(q):
         y_send(q).start()
 
     for q in (PIECES - 1, PIECES):
         y_send(q).start()
-
-    w_load = pltpu.make_async_copy(w_ref, wv, aux.at[0])
-    w_load.start()
 
     @pl.loop(0, THIRD)
     def _(q):
@@ -98,9 +107,6 @@
 
     @pl.when(diag)
     def _():
-        cp = pltpu.make_async_copy(xt_ref, xr.at[:, pl.ds(0, rows)], aux.at[1])
-        cp.start()
-
         @pl.when(z < N - 1)
         def _():
             x_up(xt_ref, 0).start()
@@ -109,7 +115,6 @@
         def _():
             x_dn(xt_ref, 0).start()
 
-        cp.wait()
         cp = pltpu.make_async_copy(xr.at[:, pl.ds(0, rows)], xg_ref.at[0], aux.at[1])
         cp.start()
         cp.wait()
@@ -121,7 +126,7 @@
 
     def x_step(c):
         for m in range(N):
-            pos = jnp.where(dist == 0, (-1, 3, 6, 7)[m], 3 * (m + dist) + (2 if m > 1 else -1))
+            pos = jnp.where(dist == 0, (-1, 3, 6, 7)[m], 3 * (m + dist) - 1)
 
             @pl.when(c == pos)
             def _():
@@ -151,20 +156,10 @@
                 for h in (0, 1)]
 
     def product(dsts, size):
-        def part(i):
-            s = pl.ds(pl.multiple_of(i * kb, kb), kb)
-            return lax.dot_general(dyv[:len(dsts) * size, s], wv[:, s], (((1,), (1,)), ((), ())),
-                                   preferred_element_type=jnp.float32)
-
-        first = part(0)
+        t = lax.dot_general(dyv[:len(dsts) * size], wv[...], (((1,), (1,)), ((), ())),
+                            preferred_element_type=jnp.float32)
         for j, d in enumerate(dsts):
-            d[...] = first[j * size:(j + 1) * size]
-
-        @pl.loop(1, 7)
-        def _(i):
-            t = part(i)
-            for j, d in enumerate(dsts):
-                d[...] += t[j * size:(j + 1) * size]
+            d[...] = t[j * size:(j + 1) * size]
 
     def rows_of(ref, c):
         if isinstance(c, int) and c >= LAST:
@@ -300,10 +295,20 @@
         ob[u % 2] = jnp.dot(xr[...], db[u % 2], preferred_element_type=jnp.float32)
         unit_out(u).start()
 
+    end_lag = jnp.where(diag, jnp.minimum(lag, 1), 0)
+    gap = lag - end_lag
+    mid_lag = jnp.where(gap >= 1, lag - 1, lag)
+
     def after(c):
-        @pl.when(c >= lag)
-        def _():
-            sum_step(c - lag)
+        now = jnp.where(c == LAST - 1, mid_lag, lag)
+
+        @pl.when(c >= now)
+        def _():
+            sum_step(c - now)
+
+        @pl.when(jnp.logical_or(jnp.logical_and(c == LAST - 2, gap >= 1), jnp.logical_and(c == LAST - 1, gap >= 2)))
+        def _():
+            sum_one(c + 1 - now)
 
     base = jnp.where(r // 2 == z // 2, 6, 3)
     ahead = PIECES - base
@@ -391,13 +396,11 @@
         for cp in load_far(q, p // 2):
             cp.wait()
         product([rows_of(pv, c)], p)
-        sum_step(c - lag)
-
-    @pl.loop(0, N - 1)
-    def _(i):
-        @pl.when(i < lag)
-        def _():
-            sum_step(CHUNKS + 1 - lag + i)
+        sum_step(c - end_lag)
+
+    @pl.when(end_lag == 1)
+    def _():
+        sum_one(LAST + 1)
 
     for u in (UNITS - 2, UNITS - 1):
         unit_out(u).wait()
@@ -471,7 +474,8 @@
         cols, s = pl.ds(pl.multiple_of(u * bn, bn), bn), lax.rem(u, SLOTS)
         return pltpu.make_async_copy(ob.at[s], dw_ref.at[:, cols], o_s.at[s])
 
-    xs = [pltpu.make_async_copy(xg_ref.at[2 + h], xr.at[:, pl.ds(h * rows, rows)], x_s.at[h]) for h in (0, 1)]
+    xs = [pltpu.make_async_copy(xg_ref.at[2 + h], xr.at[:, pl.ds(h * rows, rows)], x_s.at[h])
+          for h in (0, 1)]
     d_in = pltpu.make_async_copy(dxp_ref, dv, d_s.at[0])
     d_out = pltpu.make_async_copy(dv, dx_ref, d_s.at[1])
     for cp in xs:
@@ -515,20 +519,20 @@
 
 def solution(mesh):
     def local(x, w, dy):
-        xt = x.T
         rows, n = dy.shape
         k = w.shape[0]
         p = rows // PIECES
         dma = pltpu.SemaphoreType.DMA
         bf, f32 = jnp.bfloat16, jnp.float32
-        dx, dyg, xg, dwp = pl.pallas_call(
+        dx, dyg, xg, dwp, _ = pl.pallas_call(
             exchange,
             in_specs=[ANY] * 3,
-            out_specs=[ANY] * 4,
+            out_specs=[ANY] * 5,
             out_shape=[jax.ShapeDtypeStruct((rows, k), bf),
                        jax.ShapeDtypeStruct((N - 1, rows, n), bf),
                        jax.ShapeDtypeStruct((N, k, rows), bf),
-                       jax.ShapeDtypeStruct((k, n), f32)],
+                       jax.ShapeDtypeStruct((k, n), f32),
+                       jax.ShapeDtypeStruct((k, rows), bf)],
             scratch_shapes=[
                 pltpu.VMEM((k, n), bf), pltpu.VMEM((4 * p, n), bf),
                 pltpu.VMEM((CHUNKS, 2 * p, k), f32), pltpu.VMEM((CHUNKS, 2 * p, k), f32),
@@ -543,7 +547,7 @@
             compiler_params=pltpu.CompilerParams(collective_id=0, has_side_effects=True, vmem_limit_bytes=67043328),
             cost_estimate=pl.CostEstimate(flops=8 * rows * k * n, bytes_accessed=16 * rows * n, transcendentals=0),
             name="exchange",
-        )(xt, w, dy)
+        )(x.reshape(rows // (2 * p), 2 * p, k), w, dy)
         dw, dx = pl.pallas_call(
             finish_grads,
             in_specs=[ANY] * 4,

time: 326 us -> 319 us (0.979)
  Pallas kernels: 322 us -> 314 us
    pallas_call x1, Pallas kernels: 295 us -> 287 us  [local(): pl.pallas_call(exchange, in_specs=[ANY] * 3, out_specs=[ANY] * 5, out_sha...]
where the time goes in v3:
time: 319 us; the launch traced here: 315 us
  Pallas kernels  314 us (98%)
    pallas_call x1, Pallas kernels, local(): pl.pallas_call(exchange, in_specs=[ANY] * 3, out_specs=[ANY] * 5, out_sha...  287 us
    pallas_call x1, Pallas kernels, local(): pl.pallas_call(finish_grads, in_specs=[ANY] * 4, out_specs=[ANY] * 2, out...  27.5 us

profile of v3, /device:TPU:0, one launch (start us, length us, event | category | flops | bytes accessed | tf_op | source)
XLA Modules:
  0.0 315.2 jit_solution(9822029972334286890)
XLA Ops:
  0.6 286.8 %exchange.1 = (bf16[768,896]{1,0:T(8,128)(2,1)}, bf16[3,768,7168]{2,1,0:T(8,128)(2,1)}, bf16[4,896,768]{2,1,0:T(8,128)(2,1)}, f32[896,7168]{1,0:T(8,128)}, bf16[896,768]{1,0:T(8,128)(2,1)}) custom-call(bf16[6,128,896]{2,1,0:T(8,128)(2,1)} %bitcast.1, bf16[896,7168]{1,0:T(8,128)(2,1)} %w_ref.1, bf16[768,7168]{1,0:T(8,128)(2,1)} %dy_ref.1), custom_call_target="tpu_custom_call" | custom-call | flops 39460012032 | bytes 88080384 | tf_op jit(solution)/shard_map/exchange/pallas_call | solution.py:527
  287.5 27.5 %finish_grads.1 = (f32[896,7168]{1,0:T(8,128)}, bf16[768,896]{1,0:T(8,128)(2,1)}) custom-call(bf16[4,896,768]{2,1,0:T(8,128)(2,1)} %get-tuple-element.8.xg_ref, bf16[3,768,7168]{2,1,0:T(8,128)(2,1)} %get-tuple-element.9.dyg_ref, f32[896,7168]{1,0:T(8,128)} %get-tuple-element.10.dwp_ref, bf16[768,896]{1,0:T(8,128)(2,1)} %get-tuple-element.11.dxp_ref), custom_call_target="tpu_custom_call" | custom-call | flops 19730006016 | bytes 73400320 | tf_op jit(solution)/shard_map/finish_grads/pallas_call | solution.py:551

commit v4 on v3

--- a/solution.py
+++ b/solution.py
@@ -300,13 +300,13 @@
     mid_lag = jnp.where(gap >= 1, lag - 1, lag)
 
     def after(c):
-        now = jnp.where(c == LAST - 1, mid_lag, lag)
+        now = jnp.where(c >= LAST - 2, jnp.where(c == LAST - 2, mid_lag, end_lag), lag)
 
         @pl.when(c >= now)
         def _():
             sum_step(c - now)
 
-        @pl.when(jnp.logical_or(jnp.logical_and(c == LAST - 2, gap >= 1), jnp.logical_and(c == LAST - 1, gap >= 2)))
+        @pl.when(jnp.logical_or(jnp.logical_and(c == LAST - 3, gap >= 1), jnp.logical_and(c == LAST - 2, gap >= 2)))
         def _():
             sum_one(c + 1 - now)
 
@@ -390,11 +390,12 @@
     for c in (LAST, LAST + 1):
         q = c - PIECES
         f_step(q)
+        near, other = load_far(q, p // 2)
+        near.start()
         f_send(q).wait_recv()
-        for cp in load_far(q, p // 2):
-            cp.start()
-        for cp in load_far(q, p // 2):
-            cp.wait()
+        other.start()
+        near.wait()
+        other.wait()
         product([rows_of(pv, c)], p)
         sum_step(c - end_lag)
 

time: 319 us -> 317 us (level)
  no operation moved by 1% of the time
where the time goes in v4:
time: 317 us; the launch traced here: 315 us
  Pallas kernels  314 us (99%)
    pallas_call x1, Pallas kernels, local(): pl.pallas_call(exchange, in_specs=[ANY] * 3, out_specs=[ANY] * 5, out_sha...  287 us
    pallas_call x1, Pallas kernels, local(): pl.pallas_call(finish_grads, in_specs=[ANY] * 4, out_specs=[ANY] * 2, out...  27.5 us

profile of v4, /device:TPU:0, one launch (start us, length us, event | category | flops | bytes accessed | tf_op | source)
XLA Modules:
  0.0 315.1 jit_solution(17664249278611840192)
XLA Ops:
  0.6 286.7 %exchange.1 = (bf16[768,896]{1,0:T(8,128)(2,1)}, bf16[3,768,7168]{2,1,0:T(8,128)(2,1)}, bf16[4,896,768]{2,1,0:T(8,128)(2,1)}, f32[896,7168]{1,0:T(8,128)}, bf16[896,768]{1,0:T(8,128)(2,1)}) custom-call(bf16[6,128,896]{2,1,0:T(8,128)(2,1)} %bitcast.1, bf16[896,7168]{1,0:T(8,128)(2,1)} %w_ref.1, bf16[768,7168]{1,0:T(8,128)(2,1)} %dy_ref.1), custom_call_target="tpu_custom_call" | custom-call | flops 39460012032 | bytes 88080384 | tf_op jit(solution)/shard_map/exchange/pallas_call | solution.py:528
  287.4 27.5 %finish_grads.1 = (f32[896,7168]{1,0:T(8,128)}, bf16[768,896]{1,0:T(8,128)(2,1)}) custom-call(bf16[4,896,768]{2,1,0:T(8,128)(2,1)} %get-tuple-element.8.xg_ref, bf16[3,768,7168]{2,1,0:T(8,128)(2,1)} %get-tuple-element.9.dyg_ref, f32[896,7168]{1,0:T(8,128)} %get-tuple-element.10.dwp_ref, bf16[768,896]{1,0:T(8,128)(2,1)} %get-tuple-element.11.dxp_ref), custom_call_target="tpu_custom_call" | custom-call | flops 19730006016 | bytes 73400320 | tf_op jit(solution)/shard_map/finish_grads/pallas_call | solution.py:552
